TPU v7x, 256 devices: a whole 4x4x8 slice. The times are simulated.
256 devices in a mesh: slab: 8 (over x, core), rep: 32 (over z, y).
Axes of the slice: x: 4, y: 4, z: 8, core: 2. Of those that a mesh axis runs over, the one named last changes fastest.
Arguments:
- image: float32 [288, 256, 256], P('slab', 'rep'), may hold values from 0.5 to 2
- sensitivity: float32 [288, 256, 256], P('slab', 'rep'), may hold values from 0.5 to 2
- system_blocks: bfloat16 [4096, 128, 1024], P(('slab', 'rep')), may hold values from 0 to 0.00390625
- tile_slab: int32 [4096, 1], P(('slab', 'rep')), may hold values from 0 to 7; in each aligned block of 16 rows (0 to 15, 16 to 31, ...) at most 6 rows name the same one
- tile_block: int32 [4096], P(('slab', 'rep')), may hold values from 0 to 2303
- background: bfloat16 [4096, 128], P(('slab', 'rep')), may hold values from 0.19921875 to 1
Outputs:
- updated: float32 [288, 256, 256], P('slab', 'rep')
Inputs may be any that keep to these rules, and one draw needn't show every extreme that they name: `tile_slab`: among the 16 tiles of one device at most 6 view the same slab, and in some devices some slab is viewed by exactly 6.
All inputs are finite; a program needn't handle non-finite values.
Results may differ from a plain program's by a relative error of at most 0.0003.
Values may be sent and summed in bfloat16 or wider, within the bound.
A program may use at most 64 MiB of HBM per device.

v0:
```python
import jax
import jax.numpy as jnp
from jax import lax
from jax.sharding import Mesh
from jax.sharding import PartitionSpec as P

CAP = 6
SLAB = ("slab_0", "slab_1")
REP = ("rep_0", "rep_1")
SLAB_REP = ("slab_0", "slab_1", "rep_0", "rep_1")


def whole_of(shard, axes, dim):
    whole = shard
    for number in range(len(axes) - 1, -1, -1):
        whole = lax.all_gather(whole, axes[number], axis=dim, tiled=True)
    return whole


def split_up(shard, dim, devices):
    before, after = (shard.shape[:dim], shard.shape[dim + 1 :])
    return jnp.moveaxis(shard.reshape(*before, devices, -1, *after), dim, 0)


def joined_along(blocks, dim):
    lengths = list(blocks.shape[1:])
    lengths[dim] *= blocks.shape[0]
    return jnp.moveaxis(blocks, 0, dim).reshape(lengths)


def exchange_in_order(blocks, axes, sequence):
    inside = blocks.shape[1:]
    whole = blocks.reshape(*(lax.axis_size(a) for a in axes), *inside)
    for k in sequence:
        whole = lax.all_to_all(whole, axes[k], k, k, tiled=True)
    return whole.reshape(-1, *inside)


def stepwise_exchange(shard, axes, sequence, split_dim, concat_dim):
    blocks = split_up(shard, split_dim, lax.axis_size(axes))
    return joined_along(exchange_in_order(blocks, axes, sequence), concat_dim)


def sum_by_axis(shard, axes, dim):
    for axis in axes:
        shard = lax.psum_scatter(shard, axis, scatter_dimension=dim, tiled=True)
    return shard


def project_tiles(response_operator_lines, emission_cell_entries, back_ground):
    forward_projection = jnp.einsum(
        "qgnm,qgm->qgn",
        response_operator_lines,
        emission_cell_entries,
        preferred_element_type=jnp.float32,
    )
    inverse_permutation = (1.0 / (forward_projection + back_ground.astype(jnp.float32))).astype(
        jnp.bfloat16
    )
    return jnp.einsum(
        "uamx,uam->uax",
        response_operator_lines,
        inverse_permutation,
        preferred_element_type=jnp.float32,
    )


def local(image, sensitivity, system_blocks, tile_slab, tile_block, background):
    slab_count = lax.axis_size(SLAB)
    tiles_here, tile_rows, width = system_blocks.shape
    destination = tile_slab[:, 0]
    emission_layer_share = whole_of(image.astype(jnp.bfloat16), REP, 1)
    detector_plane_count, row_count, column_count = emission_layer_share.shape
    image_blocks = emission_layer_share.reshape(-1, width)
    block_count = image_blocks.shape[0]
    one_hot_selector = (
        destination[:, None] == jnp.arange(slab_count, dtype=jnp.int32)[None, :]
    ).astype(jnp.int32)
    position_order = jnp.sum(
        (jnp.cumsum(one_hot_selector, axis=0) - one_hot_selector) * one_hot_selector, axis=1
    )
    matches = (one_hot_selector[:, :, None] == 1) & (
        position_order[:, None, None] == jnp.arange(CAP, dtype=jnp.int32)[None, None, :]
    )
    filled = jnp.any(matches, axis=0)
    picked = jnp.sum(
        matches.astype(jnp.int32) * jnp.arange(tiles_here, dtype=jnp.int32)[:, None, None], axis=0
    )
    send_rows = jnp.where(
        filled[:, :, None, None], system_blocks[picked], jnp.zeros((), jnp.bfloat16)
    )
    send_ids = jnp.where(filled, tile_block[picked], 0)
    send_ground = jnp.where(filled[:, :, None], background[picked], jnp.ones((), jnp.bfloat16))
    holder_labels = stepwise_exchange(send_ids, SLAB, (1, 0), 0, 0)
    served_requests = image_blocks[holder_labels]
    emission_cell_entries = lax.all_to_all(
        served_requests, SLAB, split_axis=0, concat_axis=0, tiled=True
    )
    sent_back = project_tiles(send_rows, emission_cell_entries, send_ground)
    backproj = lax.all_to_all(sent_back, SLAB, split_axis=0, concat_axis=0, tiled=True)
    partial_value = (
        jnp.zeros((block_count, width), jnp.float32)
        .at[holder_labels.reshape(-1)]
        .add(backproj.reshape(-1, width))
    )
    partial_value = partial_value.reshape(detector_plane_count, row_count, column_count)
    owned = sum_by_axis(partial_value, REP, 1)
    return image * owned / sensitivity


def solution(mesh):
    finer = Mesh(mesh.devices.reshape(4, 2, 8, 4), ("slab_0", "slab_1", "rep_0", "rep_1"))
    return jax.shard_map(
        local,
        mesh=finer,
        in_specs=(
            P(SLAB, REP, None),
            P(SLAB, REP, None),
            P(SLAB_REP, None, None),
            P(SLAB_REP, None),
            P(SLAB_REP),
            P(SLAB_REP, None),
        ),
        out_specs=P(SLAB, REP, None),
        check_vma=False,
    )
```

profile of v0, /device:TPU:1, one launch (start us, length us, event | category | flops | bytes accessed | tf_op | source)
XLA Modules:
  0.0 291.5 jit_solution(212350701380922833)
XLA Ops:
  6.5 0.0 copy-start
  6.5 0.0 all-gather.2.cloned.1.call-start
  6.5 1.0 convert_element_type.18
  7.5 13.2 %all_gather.6 = bf16[36,32,256]{2,1,0:T(8,128)(2,1)} all-gather(bf16[36,8,256]{2,1,0:T(8,128)(2,1)S(1)} %convert_element_type.18), channel_id=1, replica_groups=mesh['slab_0'=4,'slab_1'=2,'rep_0'=8,'rep_1'=4] {'rep_1'}, dimensions={1}, use_global_device_ids=true | all-gather | bytes 737280 | tf_op jit(solution)/shard_map/all_gather | solution.py:16
  20.8 0.0 all-gather.2.cloned.1.call-update
  20.8 0.7 fusion.13
  21.5 0.1 copy.9
  21.7 0.8 select_reduce_fusion
  22.5 0.2 fusion.9
  22.7 0.1 copy.10
  22.8 0.1 reshape.150
  22.9 1.4 gather_fusion
  24.3 0.1 reshape.149
  24.4 0.1 copy.11
  24.5 0.2 and_reduce_fusion
  24.7 0.1 copy.12
  24.8 7.3 %all_to_all.20 = s32[4,2,1,6]{3,0,2,1:T(4,128)S(1)} all-to-all(s32[4,2,1,6]{3,0,2,1:T(4,128)S(1)} %copy.13), channel_id=1, replica_groups=mesh['slab_0'=4,'slab_1'=2,'rep_0'=8,'rep_1'=4] {'slab_1'}, dimensions={1} | all-to-all | bytes 384 | tf_op jit(solution)/shard_map/all_to_all | solution.py:35
  32.0 6.5 %all_to_all.21 = s32[4,2,1,6]{3,1,2,0:T(2,128)S(1)} all-to-all(s32[4,2,1,6]{3,1,2,0:T(2,128)S(1)} %copy.14), channel_id=1, replica_groups=mesh['slab_0'=4,'slab_1'=2,'rep_0'=8,'rep_1'=4] {'slab_0'}, dimensions={0} | all-to-all | bytes 384 | tf_op jit(solution)/shard_map/all_to_all | solution.py:35
  38.5 0.1 reshape.166
  38.6 46.6 %all-gather.2.cloned.1.call-done = bf16[36,256,256]{2,1,0:T(8,128)(2,1)} async-done(((bf16[36,32,256]{2,1,0:T(8,128)(2,1)}), bf16[36,256,256]{2,1,0:T(8,128)(2,1)}) %all-gather.2.cloned.1.call-update) | async-done | bytes 4718608 | tf_op jit(solution)/shard_map/all_gather | solution.py:16
  85.2 8.6 %reshape.145 = bf16[2304,1024]{1,0:T(8,128)(2,1)} reshape(bf16[36,256,256]{2,1,0:T(8,128)(2,1)} %all-gather.2.cloned.1.call-done) | data formatting | bytes 9437184 | tf_op jit(solution)/shard_map/reshape | solution.py:74
  93.8 3.7 %gather_fusion.2 = bf16[48,1024]{1,0:T(8,128)(2,1)S(1)} fusion(bf16[2304,1024]{1,0:T(8,128)(2,1)} %reshape.145, s32[1024]{0:T(1024)S(1)} %pad_clamp_fusion), kind=kCustom, calls=%fused_computation.2 | custom fusion | bytes 196800 | tf_op jit(solution)/shard_map/gather | solution.py:95
  97.5 0.7 reshape.165
  98.2 5.1 %all-to-all-start.2 = ((bf16[8,6,1024]{2,1,0:T(8,128)(2,1)}), bf16[8,6,1024]{2,1,0:T(8,128)(2,1)S(1)}, u32[]{:S(2)}, u32[]{:S(2)}) async-start(bf16[8,6,1024]{2,1,0:T(8,128)(2,1)} %reshape.165), calls=%async_computation.2 | async-start | bytes 262144 | tf_op jit(solution)/shard_map/all_to_all | solution.py:96
  103.3 0.1 copy.15
  103.4 0.0 copy-done
  103.4 0.6 gather_fusion.3
  104.0 8.5 %gather_fusion.1 = bf16[48,128,1024]{2,1,0:T(8,128)(2,1)} fusion(bf16[16,128,1024]{2,1,0:T(8,128)(2,1)} %param.8, s32[1024]{0:T(1024)S(1)} %pad_clamp_fusion.1), kind=kCustom, calls=%fused_computation.1 | custom fusion | bytes 25166016 | tf_op jit(solution)/shard_map/gather | solution.py:90
  112.5 0.1 reshape_reshape_reshape.3
  112.5 0.0 all-to-all-done.2
  112.6 6.4 %fusion.1 = f32[8,6,1,128]{3,2,1,0:T(1,128)S(1)} fusion(bf16[8,6,128,1024]{3,2,1,0:T(8,128)(2,1)} %bitcast.28, pred[8,6]{1,0:T(8,128)(4,1)S(1)} %copy.15, bf16[8,6,1024,1]{2,1,0,3:T(8,128)(2,1)S(1)} %bitcast.30), kind=kOutput, calls=%fused_computation.7 | convolution fusion | flops 18874368 | bytes 12705840 | tf_op jit(solution)/shard_map/qgnm,qgm->qgn/dot_general | solution.py:51
  119.0 0.1 fusion.11
  119.1 6.4 %fusion = f32[8,6,1,1024]{3,2,1,0:T(1,128)S(1)} fusion(bf16[8,6,128,1024]{3,2,1,0:T(8,128)(2,1)} %bitcast.29, pred[8,6]{1,0:T(8,128)(4,1)S(1)} %copy.15, bf16[8,6,128,1]{2,1,0,3:T(8,128)(2,1)S(1)} %fusion.11), kind=kOutput, calls=%fused_computation.6 | convolution fusion | flops 18874368 | bytes 12791856 | tf_op jit(solution)/shard_map/uamx,uam->uax/dot_general | solution.py:60
  125.5 0.8 copy.29
  126.2 4.8 %all-to-all-start.3 = ((f32[8,6,1024]{2,1,0:T(8,128)}), f32[8,6,1024]{2,1,0:T(8,128)S(1)}, u32[]{:S(2)}, u32[]{:S(2)}) async-start(f32[8,6,1024]{2,1,0:T(8,128)} %bitcast.27), calls=%async_computation.3 | async-start | bytes 524288 | tf_op jit(solution)/shard_map/all_to_all | solution.py:100
  131.0 0.0 reduce-scatter.3.cloned.1.call-start
  131.0 6.5 %all-to-all-done.3 = f32[8,6,1024]{2,1,0:T(8,128)S(1)} async-done(((f32[8,6,1024]{2,1,0:T(8,128)}), f32[8,6,1024]{2,1,0:T(8,128)S(1)}, u32[]{:S(2)}, u32[]{:S(2)}) %all-to-all-start.3) | async-done | bytes 196640 | tf_op jit(solution)/shard_map/all_to_all | solution.py:100
  137.5 5.2 %scatter_custom_fusion = f32[2304,1024]{1,0:T(8,128)} fusion(s32[48]{0:T(128)S(1)} %fusion.14, f32[48,1024]{1,0:T(8,128)S(1)} %reshape.184, f32[]{:T(128)} %constant.9.clone.1), kind=kCustom, calls=%fused_computation.10 | custom fusion | flops 49152 | bytes 9437188 | tf_op jit(solution)/shard_map/scatter-add | solution.py:104
  142.7 11.8 %reshape.147 = f32[36,256,256]{2,1,0:T(8,128)} reshape(f32[2304,1024]{1,0:T(8,128)} %scatter_custom_fusion) | data formatting | bytes 18874368 | tf_op jit(solution)/shard_map/reshape | solution.py:106
  154.6 0.0 copy-start.1
  154.6 0.0 copy-start.2
  154.6 0.0 reduce-scatter.3.cloned.1.call-update
  154.6 0.0 reduce-scatter.5.cloned.1.call-start
  154.6 102.0 %reduce-scatter.3.cloned.1.call-done = f32[36,32,256]{2,1,0:T(8,128)} async-done(((f32[36,256,256]{2,1,0:T(8,128)}), f32[36,32,256]{2,1,0:T(8,128)}) %reduce-scatter.3.cloned.1.call-update) | async-done | bytes 1179664 | tf_op jit(solution)/shard_map/reduce_scatter | solution.py:46
  256.7 0.0 reduce-scatter.5.cloned.1.call-update
  256.7 26.6 %reduce-scatter.5.cloned.1.call-done = f32[36,8,256]{2,1,0:T(8,128)} async-done(((f32[36,32,256]{2,1,0:T(8,128)}), f32[36,8,256]{2,1,0:T(8,128)}) %reduce-scatter.5.cloned.1.call-update) | async-done | bytes 294928 | tf_op jit(solution)/shard_map/reduce_scatter | solution.py:46
  283.3 0.0 copy-done.1
  283.3 0.0 copy-done.2
  283.3 1.8 multiply_divide_fusion
  (12 shorter events, 0.1 us)
Async XLA Ops:
  6.5 96.8 %copy-start = (bf16[16,128]{1,0:T(8,128)(2,1)S(1)}, bf16[16,128]{1,0:T(8,128)(2,1)}, u32[]{:S(2)}) copy-start(bf16[16,128]{1,0:T(8,128)(2,1)} %param.11) | copy-start | bytes 12292
  6.5 78.7 %all-gather.2.cloned.1.call-start = ((), (), s32[]{:S(2)}) async-start(), calls=%async_computation.6 | async-start | bytes 5308416 | tf_op jit(solution)/shard_map/all_gather | solution.py:16
  98.2 14.4 %all-to-all-start.2 = ((bf16[8,6,1024]{2,1,0:T(8,128)(2,1)}), bf16[8,6,1024]{2,1,0:T(8,128)(2,1)S(1)}, u32[]{:S(2)}, u32[]{:S(2)}) async-start(bf16[8,6,1024]{2,1,0:T(8,128)(2,1)} %reshape.165), calls=%async_computation.2 | async-start | bytes 262144 | tf_op jit(solution)/shard_map/all_to_all | solution.py:96
  126.2 11.3 %all-to-all-start.3 = ((f32[8,6,1024]{2,1,0:T(8,128)}), f32[8,6,1024]{2,1,0:T(8,128)S(1)}, u32[]{:S(2)}, u32[]{:S(2)}) async-start(f32[8,6,1024]{2,1,0:T(8,128)} %bitcast.27), calls=%async_computation.3 | async-start | bytes 524288 | tf_op jit(solution)/shard_map/all_to_all | solution.py:100
  131.0 125.6 %reduce-scatter.3.cloned.1.call-start = ((), (), s32[]{:S(2)}) async-start(), calls=%async_computation.7 | async-start | bytes 10616832 | tf_op jit(solution)/shard_map/reduce_scatter | solution.py:46
  154.6 128.7 %copy-start.1 = (f32[36,8,256]{2,1,0:T(8,128)S(1)}, f32[36,8,256]{2,1,0:T(8,128)}, u32[]{:S(2)}) copy-start(f32[36,8,256]{2,1,0:T(8,128)} %param.6) | copy-start | bytes 884740
  154.6 128.7 %copy-start.2 = (f32[36,8,256]{2,1,0:T(8,128)S(1)}, f32[36,8,256]{2,1,0:T(8,128)}, u32[]{:S(2)}) copy-start(f32[36,8,256]{2,1,0:T(8,128)} %param.7) | copy-start | bytes 884740
  154.6 128.7 %reduce-scatter.5.cloned.1.call-start = ((), (), s32[]{:S(2)}) async-start(), calls=%async_computation.8 | async-start | bytes 1474560 | tf_op jit(solution)/shard_map/reduce_scatter | solution.py:46
Sparse Core Ops, SparseCore 0:
  20.9 64.2 all-gather.1
  154.7 101.9 reduce-scatter.2
  259.2 23.9 reduce-scatter.4
where the time goes:
time: 293 us; the launch traced here: 292 us
  waiting for transfers between devices  182 us (62%)
  local copies, waits for them, and re-layouts  36.9 us (13%)
  blocking collectives  27 us (9%)
  between operations  13.2 us (5%)
  matrix products  12.8 us (4%)
  other arithmetic  10.1 us (3%)
  starting transfers between devices  9.94 us (3%)
    reduce_scatter x2, waiting for transfers between devices, sum_by_axis(): shard = lax.psum_scatter(shard, axis, scatter_dimension=dim, tiled=True)  129 us
    all_gather x1, waiting for transfers between devices, whole_of(): whole = lax.all_gather(whole, axes[number], axis=dim, tiled=True)  46.6 us
    all_to_all x2, blocking collectives, exchange_in_order(): whole = lax.all_to_all(whole, axes[k], k, k, tiled=True)  13.7 us
    all_gather x1, blocking collectives, whole_of(): whole = lax.all_gather(whole, axes[number], axis=dim, tiled=True)  13.2 us
    reshape x1, local copies, waits for them, and re-layouts, local(): partial_value.reshape(detector_plane_count, row_count, column_count)  11.8 us
    reshape x1, local copies, waits for them, and re-layouts, local(): image_blocks = emission_layer_share.reshape(-1, width)  8.57 us
    gather x1, local copies, waits for them, and re-layouts, local(): system_blocks[picked]  8.46 us
    all_to_all x1, waiting for transfers between devices, local(): lax.all_to_all(sent_back, SLAB, split_axis=0, concat_axis=0, tiled=True)  6.46 us
  transfers between devices with their start and end apart: 5, of which 4 were waited for; matrix products, arithmetic and copies ran while one was open for 5% of the time, Pallas kernels for 0%

commit v1 on v0

v1 whole, which is shorter than its diff:
```python
import functools

import jax
import jax.numpy as jnp
from jax import lax
from jax.experimental import pallas as pl
from jax.experimental.pallas import tpu as pltpu
from jax.sharding import Mesh
from jax.sharding import PartitionSpec as P

SLAB = ("x", "core")
REP = ("z", "y")
ALL = ("x", "core", "z", "y")
MESH = pl.DeviceIdType.MESH
F32, BF16, I32 = jnp.float32, jnp.bfloat16, jnp.int32
VB = 1024
PER = 8
CAP = 6
ROUND = 16
SUBS = 4


def iota(shape, axis):
    return lax.broadcasted_iota(I32, shape, axis)


def log2(n):
    assert n & (n - 1) == 0
    return n.bit_length() - 1


def split3(value):
    high = value.astype(BF16)
    rest = value - high.astype(F32)
    middle = rest.astype(BF16)
    low = (rest - middle.astype(F32)).astype(BF16)
    return high, middle, low


def column_of(row, eye):
    return jnp.sum(jnp.where(eye, row, 0.0), axis=1, keepdims=True)


def row_of(column, eye):
    return jnp.sum(jnp.where(eye, column, 0.0), axis=0, keepdims=True)


def kernel(
    sizes, nloc, tiles,
    round_ref, image_ref, slab_ref, block_ref, ground_ref, system_hbm, sens_hbm,
    out_ref, most_ref,
    system, sens, left, right, chunks, ask, asked, acc, wide, fetch, got, back, came, zsend, zcame,
    sem_local, s_chunk, r_chunk, s_ask, r_ask, s_fetch, r_fetch, s_back, r_back, s_z, r_z,
):
    nx, nc, nz, ny = sizes
    plane = nx * nc * ny
    rows = plane * PER
    half = nz // 2
    sub = VB // SUBS
    x, core, z, y = (lax.axis_index(a) for a in ALL)
    me = (x * nc + core) * ny + y

    def at(q):
        return (q // (nc * ny), (q // ny) % nc, z, q % ny)

    def along(step):
        return (x, core, (z + step) % nz, y)

    load_system = pltpu.make_async_copy(system_hbm, system, sem_local.at[0])
    load_sens = pltpu.make_async_copy(sens_hbm, sens, sem_local.at[1])
    load_system.start()
    load_sens.start()

    barrier = pltpu.get_barrier_semaphore()
    for step in range(1, nz):
        pl.semaphore_signal(barrier, inc=1, device_id=along(step), device_id_type=MESH)

    def greet(k, carry):
        pl.semaphore_signal(barrier, inc=1, device_id=at((me + k) % plane), device_id_type=MESH)
        return carry

    lax.fori_loop(1, plane, greet, 0)

    left[...] = image_ref[:, :128]
    right[...] = image_ref[:, 128:]
    for a in range(8):
        side = right if a % 2 else left
        piece = side[pl.ds(a // 2, nloc, stride=4), :]
        chunks[0, :, pl.ds(a * 128, 128)] = piece.astype(BF16)

    eye = iota((tiles, tiles), 0) == iota((tiles, tiles), 1)
    per_plane = 2 * nz * ny
    block = column_of(block_ref[...].astype(F32), eye).astype(I32)
    rep = jnp.right_shift(block & (per_plane - 1), 1)
    ztile = jnp.right_shift(rep, log2(ny))
    place = jnp.right_shift(block, log2(per_plane)) * 2 + (block & 1)
    partner = slab_ref[...] * ny + (rep & (ny - 1))
    index_col = (ztile * nloc + place + 1).astype(F32)
    code_col = (partner * nz + ztile + 1).astype(F32)
    partner_col = partner.astype(F32)
    partner_row = row_of(partner_col, eye)
    before = (partner_col == partner_row) & (iota((tiles, tiles), 0) < iota((tiles, tiles), 1))
    slot_row = partner_row * PER + jnp.sum(jnp.where(before, 1.0, 0.0), axis=0, keepdims=True)
    slot_col = column_of(slot_row, eye)
    index_row = row_of(index_col, eye)
    wide_eye = iota((tiles, 128), 0) == iota((tiles, 128), 1)
    code_row = row_of(code_col, wide_eye)
    hit = iota((rows, tiles), 0).astype(F32) == slot_row
    wanted = jnp.sum(jnp.where(hit, index_row, 0.0), axis=1, keepdims=True)
    is_code = (iota((rows, 128), 0) & (PER - 1)) == CAP
    ask[...] = jnp.where(is_code, code_row, wanted)

    for q in range(plane):
        dead = pl.ds(q * PER * 8 + CAP * 8, (PER - CAP) * 8)
        wide[dead, :] = jnp.zeros(((PER - CAP) * 8, 128), F32)
        came[dead, :] = jnp.zeros(((PER - CAP) * 8, 128), F32)

    pl.semaphore_wait(barrier, plane - 1 + nz - 1)

    def pieces(direction, step):
        if step < half:
            return range(SUBS)
        return range(SUBS // 2) if direction == 0 else range(SUBS // 2, SUBS)

    def chunk_copy(direction, step, k):
        if direction == 0:
            source, target = step - 1, step
        else:
            source, target = (nz - (step - 1)) % nz, nz - step
        lanes = pl.ds(k * sub, sub)
        return pltpu.make_async_remote_copy(
            src_ref=chunks.at[source, :, lanes],
            dst_ref=chunks.at[target, :, lanes],
            send_sem=s_chunk.at[direction, step - 1, k],
            recv_sem=r_chunk.at[direction, step - 1, k],
            device_id=along(1 if direction == 0 else nz - 1),
            device_id_type=MESH,
        )

    for k in range(SUBS):
        for direction in range(2):
            if k in pieces(direction, 1):
                chunk_copy(direction, 1, k).start()

    def slab_rows(q, count):
        return pl.ds(pl.multiple_of(q * PER * 8, PER * 8), count)

    def ask_rows(q):
        return pl.ds(pl.multiple_of(q * PER, PER), PER)

    def ask_copy(q, there):
        return pltpu.make_async_remote_copy(
            src_ref=ask.at[ask_rows(q), :],
            dst_ref=asked.at[ask_rows(there), :],
            send_sem=s_ask.at[q],
            recv_sem=r_ask.at[there],
            device_id=at(q),
            device_id_type=MESH,
        )

    def fetch_copy(q, there):
        return pltpu.make_async_remote_copy(
            src_ref=fetch.at[q],
            dst_ref=got.at[there],
            send_sem=s_fetch.at[q],
            recv_sem=r_fetch.at[there],
            device_id=at(q),
            device_id_type=MESH,
        )

    def back_copy(q, there):
        return pltpu.make_async_remote_copy(
            src_ref=back.at[slab_rows(q, CAP * 8), :],
            dst_ref=came.at[slab_rows(there, CAP * 8), :],
            send_sem=s_back.at[q],
            recv_sem=r_back.at[there],
            device_id=at(q),
            device_id_type=MESH,
        )

    def each_partner(body):
        def step(k, carry):
            body((me + k) % plane)
            return carry

        lax.fori_loop(1, plane, step, 0)

    each_partner(lambda q: ask_copy(q, me).start())
    asked[ask_rows(me), :] = ask[ask_rows(me), :]

    def arrive(step):
        for k in range(SUBS):
            for direction in range(2):
                if k in pieces(direction, step):
                    chunk_copy(direction, step, k).wait_recv()
                    if step < half and k in pieces(direction, step + 1):
                        chunk_copy(direction, step + 1, k).start()

    def add_chunk(slot, first):
        base = ((z + nz - slot) % nz) * nloc + 1
        column = iota((rows, nloc), 1) + base
        pick = jnp.where(asked[:, :nloc] == column.astype(F32), 1.0, 0.0).astype(BF16)
        value = jnp.dot(pick, chunks[slot], preferred_element_type=F32)
        if first:
            acc[...] = value
        else:
            acc[...] += value

    arrive(1)
    each_partner(lambda q: ask_copy(q, q).wait_recv())
    add_chunk(0, True)
    for step in range(1, half + 1):
        if step > 1:
            arrive(step)
        add_chunk(step, False)
        if step < half:
            add_chunk(nz - step, False)

    for a in range(8):
        back[pl.ds(a, rows, stride=8), :] = acc[:, pl.ds(a * 128, 128)]

    def send_blocks(q):
        fetch[q] = back[slab_rows(q, CAP * 8), :].astype(BF16)
        fetch_copy(q, me).start()

    each_partner(send_blocks)
    got[me] = back[slab_rows(me, CAP * 8), :].astype(BF16)

    codes = asked[pl.ds(CAP, plane, stride=PER), :]
    bins = plane * nz
    count = jnp.zeros((plane, bins), F32)
    for j in range(tiles):
        match = codes[:, j : j + 1] == (iota((plane, bins), 1) + 1).astype(F32)
        count = count + jnp.where(match, 1.0, 0.0)
    most = jnp.max(jnp.sum(count, axis=0, keepdims=True), axis=1, keepdims=True)

    width = max(rows, 128)
    strips = []
    for b in range(width // 128):
        tall = min(128, rows)
        part = asked[pl.ds(b * 128, tall), :]
        live = (iota((tall, 128), 0) & (PER - 1)) < CAP
        strips.append(row_of(part, (iota((tall, 128), 0) == iota((tall, 128), 1)) & live))
    owner_row = (strips[0] if len(strips) == 1 else jnp.concatenate(strips, axis=1))[:, :rows]

    each_partner(lambda q: fetch_copy(q, q).wait_recv())

    def widen(q, carry):
        wide[slab_rows(q, CAP * 8), :] = got[q].astype(F32)
        return carry

    lax.fori_loop(0, plane, widen, 0)
    table = jnp.concatenate(
        [wide[pl.ds(a, rows, stride=8), :].astype(BF16) for a in range(8)], axis=1
    )
    mine = jnp.where(iota((tiles, rows), 1).astype(F32) == slot_col, 1.0, 0.0).astype(BF16)
    blocks = jnp.dot(mine, table, preferred_element_type=F32).astype(BF16)

    load_system.wait()
    tile_row = iota((tiles, 128), 0)
    forward = jnp.zeros((tiles, 128), F32)
    for j in range(tiles):
        value = lax.dot_general(
            blocks, system[j], (((1,), (1,)), ((), ())), preferred_element_type=F32
        )
        forward = jnp.where(tile_row == j, value, forward)
    inverse = (1.0 / (forward + ground_ref[...].astype(F32))).astype(BF16)
    wide_row = iota((tiles, VB), 0)
    result = jnp.zeros((tiles, VB), F32)
    for j in range(tiles):
        value = jnp.dot(inverse, system[j], preferred_element_type=F32)
        result = jnp.where(wide_row == j, value, result)

    eye3 = (iota((tiles, 3 * tiles), 1) & (tiles - 1)) == iota((tiles, 3 * tiles), 0)
    put = jnp.where(iota((rows, 3 * tiles), 0).astype(F32) == row_of(slot_col, eye3), 1.0, 0.0)
    parts = jnp.concatenate(split3(result), axis=0)
    acc[...] = jnp.dot(put.astype(BF16), parts, preferred_element_type=F32)
    for a in range(8):
        back[pl.ds(a, rows, stride=8), :] = acc[:, pl.ds(a * 128, 128)]
    each_partner(lambda q: back_copy(q, me).start())
    came[slab_rows(me, CAP * 8), :] = back[slab_rows(me, CAP * 8), :]

    step_col = iota((nz, rows), 0)
    zdest = jnp.where(step_col + z >= nz, step_col + z - nz, step_col + z)
    low = (zdest * nloc + 1).astype(F32)
    goes = (owner_row >= low) & (owner_row < low + nloc)
    earlier = jnp.where(iota((rows, rows), 0) < iota((rows, rows), 1), 1.0, 0.0).astype(BF16)
    goes_one = jnp.where(goes, 1.0, 0.0)
    rank = jnp.dot(goes_one.astype(BF16), earlier, preferred_element_type=F32)
    rank = rank - (round_ref[0] * ROUND).astype(F32)
    order = iota((ROUND, rows), 0).astype(F32)
    picks, places = [], []
    for step in range(nz):
        chosen = (rank[step : step + 1, :] == order) & (goes_one[step : step + 1, :] > 0.5)
        picks.append(jnp.where(chosen, 1.0, 0.0))
        places.append(jnp.where(chosen, owner_row - low[step : step + 1, :] + 1.0, 0.0))
    pick = jnp.concatenate(picks, axis=0).astype(BF16)
    where = jnp.sum(jnp.concatenate(places, axis=0), axis=1, keepdims=True)
    tagged = where + most * 128.0

    each_partner(lambda q: back_copy(q, q).wait_recv())
    value = jnp.concatenate([came[pl.ds(a, rows, stride=8), :] for a in range(8)], axis=1)
    pick3 = jnp.concatenate([pick, pick, pick], axis=1)
    packed = jnp.dot(
        pick3, jnp.concatenate(split3(value), axis=0), preferred_element_type=F32
    )
    zsend[:, :VB] = packed
    zsend[:, VB:] = jnp.broadcast_to(tagged, (nz * ROUND, 128))

    def z_copy(step):
        own = pl.ds(step * ROUND, ROUND)
        return pltpu.make_async_remote_copy(
            src_ref=zsend.at[own, :],
            dst_ref=zcame.at[own, :],
            send_sem=s_z.at[step],
            recv_sem=r_z.at[step],
            device_id=along(step),
            device_id_type=MESH,
        )

    for step in range(1, nz):
        z_copy(step).start()
    zcame[pl.ds(0, ROUND), :] = zsend[pl.ds(0, ROUND), :]
    load_sens.wait()
    for step in range(1, nz):
        z_copy(step).wait_recv()

    tags = zcame[:, VB:]
    most_all = jnp.floor(tags * (1.0 / 128.0))
    spot = tags - most_all * 128.0
    count_z = nz * ROUND
    spot_row = row_of(spot, iota((count_z, 128), 0) == iota((count_z, 128), 1))[:, :count_z]
    lands = jnp.where((iota((nloc, count_z), 0) + 1).astype(F32) == spot_row, 1.0, 0.0).astype(BF16)
    partial = jnp.dot(
        jnp.concatenate([lands, lands, lands], axis=1),
        jnp.concatenate(split3(zcame[:, :VB]), axis=0),
        preferred_element_type=F32,
    )
    for a in range(8):
        side = right if a % 2 else left
        side[pl.ds(a // 2, nloc, stride=4), :] = partial[:, a * 128 : (a + 1) * 128]
    for t, side in enumerate((left, right)):
        lanes = pl.ds(t * 128, 128)
        out_ref[:, lanes] = image_ref[:, lanes] * side[...] / sens[:, lanes]
    largest = jnp.max(jnp.max(most_all, axis=0, keepdims=True), axis=1, keepdims=True)
    most_ref[...] = jnp.broadcast_to(largest, (8, 128))

    for direction in range(2):
        for step in range(1, half + 1):
            for k in pieces(direction, step):
                chunk_copy(direction, step, k).wait_send()

    def drain(q):
        ask_copy(q, me).wait_send()
        fetch_copy(q, me).wait_send()
        back_copy(q, me).wait_send()

    each_partner(drain)
    for step in range(1, nz):
        z_copy(step).wait_send()


def update_round(sizes, number, image, slab, block, ground, system, sens):
    nx, nc, nz, ny = sizes
    plane = nx * nc * ny
    rows = plane * PER
    tiles = system.shape[0]
    lines = image.shape[0]
    nloc = lines // 4
    half = nz // 2
    dma = pltpu.SemaphoreType.DMA
    vmem = pl.BlockSpec(memory_space=pltpu.VMEM)
    return pl.pallas_call(
        functools.partial(kernel, sizes, nloc, tiles),
        out_shape=(
            jax.ShapeDtypeStruct(image.shape, F32),
            jax.ShapeDtypeStruct((8, 128), F32),
        ),
        in_specs=[
            pl.BlockSpec(memory_space=pltpu.SMEM),
            vmem, vmem, vmem, vmem,
            pl.BlockSpec(memory_space=pl.ANY),
            pl.BlockSpec(memory_space=pl.ANY),
        ],
        out_specs=(vmem, vmem),
        scratch_shapes=[
            pltpu.VMEM(system.shape, BF16),
            pltpu.VMEM(image.shape, F32),
            pltpu.VMEM((lines, 128), F32),
            pltpu.VMEM((lines, 128), F32),
            pltpu.VMEM((nz, nloc, VB), BF16),
            pltpu.VMEM((rows, 128), F32),
            pltpu.VMEM((rows, 128), F32),
            pltpu.VMEM((rows, VB), F32),
            pltpu.VMEM((rows * 8, 128), F32),
            pltpu.VMEM((plane, CAP * 8, 128), BF16),
            pltpu.VMEM((plane, CAP * 8, 128), BF16),
            pltpu.VMEM((rows * 8, 128), F32),
            pltpu.VMEM((rows * 8, 128), F32),
            pltpu.VMEM((nz * ROUND, VB + 128), F32),
            pltpu.VMEM((nz * ROUND, VB + 128), F32),
            dma((2,)),
            dma((2, half, SUBS)),
            dma((2, half, SUBS)),
            dma((plane,)), dma((plane,)),
            dma((plane,)), dma((plane,)),
            dma((plane,)), dma((plane,)),
            dma((nz,)), dma((nz,)),
        ],
        compiler_params=pltpu.CompilerParams(
            collective_id=0, has_side_effects=True, vmem_limit_bytes=48 * 1024 * 1024
        ),
        name="osem_round",
    )(number, image, slab, block, ground, system, sens)


def local(sizes, image, sensitivity, system_blocks, tile_slab, tile_block, background):
    lines = image.shape[0] * image.shape[1]
    flat = image.reshape(lines, image.shape[2])
    rest = (
        flat, tile_slab, tile_block.reshape(1, -1), background, system_blocks,
        sensitivity.reshape(flat.shape),
    )
    first, most = update_round(sizes, jnp.zeros((1,), I32), *rest)
    needed = most[0, 0].astype(I32)

    def more(total):
        def body(state):
            number, total = state
            extra, _ = update_round(sizes, jnp.full((1,), number, I32), *rest)
            return number + 1, total + extra

        return lax.while_loop(lambda s: s[0] * ROUND < needed, body, (jnp.int32(1), total))[1]

    updated = lax.cond(needed > ROUND, more, lambda total: total, first)
    return updated.reshape(image.shape)


def solution(mesh):
    finer = Mesh(mesh.devices.reshape(4, 2, 8, 4), ALL)
    return jax.shard_map(
        functools.partial(local, (4, 2, 8, 4)),
        mesh=finer,
        in_specs=(
            P(SLAB, REP, None),
            P(SLAB, REP, None),
            P(SLAB + REP, None, None),
            P(SLAB + REP, None),
            P(SLAB + REP),
            P(SLAB + REP, None),
        ),
        out_specs=P(SLAB, REP, None),
        check_vma=False,
    )
```

time: 293 us -> 69.6 us (0.24)
  waiting for transfers between devices: 182 us -> 0 us
  Pallas kernels: 0 us -> 66.7 us
  local copies, waits for them, and re-layouts: 36.9 us -> 2.05 us
  blocking collectives: 27 us -> 0 us
  matrix products: 12.8 us -> 0 us
  between operations: 13.2 us -> 0.73 us
  other arithmetic: 10.1 us -> 0 us
  starting transfers between devices: 9.94 us -> 0 us
    reduce_scatter x2 -> x0, waiting for transfers between devices: 129 us -> none  [sum_by_axis(): shard = lax.psum_scatter(shard, axis, scatter_dimension=dim, tiled=True)]
    pallas_call x0 -> x1, Pallas kernels: none -> 66.7 us  [update_round(): pl.pallas_call(functools.partial(kernel, sizes, nloc, tiles), out_shape=(...]
    all_gather x1 -> x0, waiting for transfers between devices: 46.6 us -> none  [whole_of(): whole = lax.all_gather(whole, axes[number], axis=dim, tiled=True)]
    reshape x3 -> x0, local copies, waits for them, and re-layouts: 20.4 us -> none  [the longest x1 11.8 us: local(): partial_value.reshape(detector_plane_count, row_count, column_count)]
    gather x8 -> x0, local copies, waits for them, and re-layouts: 15 us -> none  [the longest x1 8.46 us: local(): system_blocks[picked]]
    all_to_all x2 -> x0, blocking collectives: 13.7 us -> none  [exchange_in_order(): whole = lax.all_to_all(whole, axes[k], k, k, tiled=True)]
    all_gather x1 -> x0, blocking collectives: 13.2 us -> none  [whole_of(): whole = lax.all_gather(whole, axes[number], axis=dim, tiled=True)]
    dot_general x2 -> x0, matrix products: 12.8 us -> none  [the longest x1 6.43 us: project_tiles(): jnp.einsum('qgnm,qgm->qgn', response_operator_lines, emission_cell_entrie...]
  transfers between devices with their start and end apart: 5 -> 0, of which waited for: 4 -> 0; matrix products, arithmetic and copies ran while one was open for 5% -> 0% of each run, Pallas kernels for 0% -> 0%
where the time goes in v1:
time: 69.6 us; the launch traced here: 69.5 us
  Pallas kernels  66.7 us (96%)
  local copies, waits for them, and re-layouts  2.05 us (3%)
  between operations  0.73 us (1%)
    pallas_call x1, Pallas kernels, update_round(): pl.pallas_call(functools.partial(kernel, sizes, nloc, tiles), out_shape=(...  66.7 us
    unnamed x12, local copies, waits for them, and re-layouts  1.54 us

profile of v1, /device:TPU:1, one launch (start us, length us, event | category | flops | bytes accessed | tf_op | source)
XLA Modules:
  0.0 69.5 jit_solution(9398335281938969180)
XLA Ops:
  0.0 0.0 copy-start.2
  0.0 0.0 copy-start.4
  0.0 0.0 copy-start.3
  0.0 0.0 copy-start.1
  0.0 0.0 copy-start
  0.0 0.8 %copy.9.slab_ref = s32[16,1]{1,0:T(8,128)S(1)} copy(s32[16,1]{0,1:T(1,128)} %param.13) | data formatting | bytes 128 | tf_op args[3]
  0.8 66.7 %osem_round.2 = (f32[288,256]{1,0:T(8,128)S(1)}, f32[8,128]{1,0:T(8,128)S(1)}) custom-call(s32[1]{0:T(128)} %constant.3.clone.1.round_ref, f32[288,256]{1,0:T(8,128)} %bitcast.9, s32[16,1]{1,0:T(8,128)S(1)} %copy.9.slab_ref, s32[1,16]{1,0:T(1,128)} %bitcast.15, bf16[16,128]{1,0:T(8,128)(2,1)} %ground_ref.1, bf16[16,128,1024]{2,1,0:T(8,128)(2,1)} %system_hbm.1, ...), custom_call_target="tpu_custom_call" | custom-call | tf_op jit(solution)/shard_map/osem_round/pallas_call | solution.py:373
  67.6 0.5 slice.3
  68.7 0.0 copy-done.2
  68.7 0.0 copy-done.4
  68.7 0.0 copy-done.3
  68.8 0.0 copy-done.1
  68.8 0.0 copy-done
  68.8 0.7 %copy.21 = f32[36,8,256]{2,1,0:T(8,128)} copy(f32[36,8,256]{2,1,0:T(8,128)S(1)} %get-tuple-element.88) | data formatting | bytes 589824
  (1 shorter events, 0.0 us)
Async XLA Ops:
  0.0 68.7 %copy-start.2 = (bf16[16,128]{1,0:T(8,128)(2,1)S(1)}, bf16[16,128]{1,0:T(8,128)(2,1)}, u32[]{:S(2)}) copy-start(bf16[16,128]{1,0:T(8,128)(2,1)} %ground_ref.1) | copy-start | bytes 12292
  0.0 68.7 %copy-start.4 = (s32[16,1]{0,1:T(1,128)S(1)}, s32[16,1]{0,1:T(1,128)}, u32[]{:S(2)}) copy-start(s32[16,1]{0,1:T(1,128)} %param.13) | copy-start | bytes 196
  0.0 68.7 %copy-start.3 = (s32[16]{0:T(128)S(1)}, s32[16]{0:T(128)}, u32[]{:S(2)}) copy-start(s32[16]{0:T(128)} %param.14) | copy-start | bytes 196
  0.0 68.7 %copy-start.1 = (f32[36,8,256]{2,1,0:T(8,128)S(1)}, f32[36,8,256]{2,1,0:T(8,128)}, u32[]{:S(2)}) copy-start(f32[36,8,256]{2,1,0:T(8,128)} %param.11) | copy-start | bytes 884740
  0.0 68.7 %copy-start = (f32[36,8,256]{2,1,0:T(8,128)S(1)}, f32[36,8,256]{2,1,0:T(8,128)}, u32[]{:S(2)}) copy-start(f32[36,8,256]{2,1,0:T(8,128)} %param.10) | copy-start | bytes 884740
